TPU v7x, 32 devices: a whole 2x2x4 slice. The times are simulated.
32 devices in a mesh: shell: 2 (over x), pix: 16 (over z, y, core).
Axes of the slice: x: 2, y: 2, z: 4, core: 2. Of those that a mesh axis runs over, the one named last changes fastest.
Arguments:
- block_tile: int32 [4, 1024], P('shell'), may hold values from 0 to 2047, as said below
- cell_index: int32 [4, 1024, 512], P('shell', 'pix'), may hold values from 0 to 2047
- masses: bfloat16 [4, 1024, 512], P('shell', 'pix'), may hold values from 0.125 to 8, as said below
- plane_coef: float32 [4], P('shell'), may hold values from 0.1 to 0.4
- plane_dist: float32 [4], P('shell'), may hold values from 0.2 to 1
- source_inv: float32 [4], P('shell'), may hold values from 0.5 to 1
Outputs:
- convergence: float32 [4, 2048, 2048], P('shell', 'pix')
- shear_one: float32 [4, 2048, 2048], P('shell', 'pix')
- shear_two: float32 [4, 2048, 2048], P('shell', 'pix')
Inputs may be any that keep to these rules, and one draw needn't show every extreme that they name: `block_tile`: each row is 16 aligned runs of 64 entries, one run per index of pix. The entries of a run are distinct, and at most 8 of them lie in one index's rows of tiles (tile b lies in the rows of index b // 128). In every plane some index receives exactly 8 tiles from every run. `masses`: positive particle weights.
All inputs are finite; a program needn't handle non-finite values.
Results may differ from a plain program's by a relative error of at most 0.0003.
Values sent between devices are 32-bit elements; how exact they have to be, the bound alone decides.
A program may use at most 64 MiB of HBM per device.

v0:
```python
from functools import partial
import math
import jax
import jax.numpy as jnp
from jax import lax
from jax.sharding import PartitionSpec as P

L = 2048
TR = 16
TC = 128
HIGHEST = lax.Precision.HIGHEST


def entering(value, axis, join, neutral):
    count, mine = (lax.axis_size(axis), lax.axis_index(axis))
    pieces = jax.tree.map(lambda part: lax.all_gather(part, axis), value)
    running = jax.tree.map(
        lambda part, zero: jnp.full_like(part, 0) + jnp.asarray(zero, part.dtype), value, neutral
    )

    def lap(position, running):
        longer = join(running, jax.tree.map(lambda part: part[position], pieces))
        return jax.tree.map(lambda new, old: jnp.where(position < mine, new, old), longer, running)

    return lax.fori_loop(0, count - 1, lap, running)


def dft_table(left_size, right_size, period, sign_value):
    left_idx = jnp.arange(left_size)[:, None]
    right_idx = jnp.arange(right_size)[None, :]
    angle = 2.0 * math.pi / period * (left_idx * right_idx % period).astype(jnp.float32)
    return (jnp.cos(angle), sign_value * jnp.sin(angle))


def mix_outer(table, real_part, imag_part):
    cosine, sine_part = table
    contract = partial(jnp.einsum, "ab,...bc->...ac", precision=HIGHEST)
    return (
        contract(cosine, real_part) - contract(sine_part, imag_part),
        contract(sine_part, real_part) + contract(cosine, imag_part),
    )


def mix_inner(table, real_part, imag_part):
    cosine, sine_part = table
    product = partial(jnp.matmul, precision=HIGHEST)
    return (
        product(real_part, cosine) - product(imag_part, sine_part),
        product(real_part, sine_part) + product(imag_part, cosine),
    )


def twist(table, real_part, imag_part):
    cosine, sine_part = table
    return (real_part * cosine - imag_part * sine_part, real_part * sine_part + imag_part * cosine)


def transform_last(real_part, imag_part, sign_value):
    length = real_part.shape[-1]
    inner = math.gcd(length, 128)
    outer = length // inner
    leading = real_part.shape[:-1]
    real_part = real_part.reshape(leading + (outer, inner))
    imag_part = imag_part.reshape(leading + (outer, inner))
    outer_table = dft_table(outer, outer, outer, sign_value)
    inner_table = dft_table(inner, inner, inner, sign_value)
    twiddle = dft_table(outer, inner, length, sign_value)
    if sign_value < 0:
        real_part, imag_part = mix_outer(outer_table, real_part, imag_part)
        real_part, imag_part = twist(twiddle, real_part, imag_part)
        real_part, imag_part = mix_inner(inner_table, real_part, imag_part)
    else:
        real_part, imag_part = mix_inner(inner_table, real_part, imag_part)
        real_part, imag_part = twist(twiddle, real_part, imag_part)
        real_part, imag_part = mix_outer(outer_table, real_part, imag_part)
    return (real_part.reshape(leading + (length,)), imag_part.reshape(leading + (length,)))


def frequency_of(position, length):
    inner = math.gcd(length, 128)
    outer = length // inner
    frequency = position // inner + outer * (position % inner)
    signed = jnp.where(frequency >= length // 2, frequency - length, frequency).astype(jnp.float32)
    keep_mask = (frequency != length // 2).astype(jnp.float32)
    return (signed, keep_mask)


def add_pairs(earlier_pair, later_pair):
    return (earlier_pair[0] + later_pair[0], earlier_pair[1] + later_pair[1])


def deposit_group(item):
    cell_ids, weights = item
    tile_rows = cell_ids // TC
    tile_cols = cell_ids % TC
    row_hot = jnp.where(
        tile_rows[:, None, :] == jnp.arange(TR)[None, :, None],
        weights[:, None, :],
        jnp.zeros((), jnp.bfloat16),
    )
    col_hot = (tile_cols[:, :, None] == jnp.arange(TC)[None, None, :]).astype(jnp.bfloat16)
    return jnp.einsum("grk,gkc->grc", row_hot, col_hot, preferred_element_type=jnp.float32)


def rows_to_sending(packed, groups, slab, cols_own):
    count, fields = (packed.shape[0], packed.shape[1])
    return (
        packed.reshape(count, fields, slab, groups, cols_own)
        .transpose(3, 0, 1, 4, 2)
        .reshape(groups, count, fields, cols_own * slab)
    )


def arrived_to_columns(arrived, groups, slab, cols_own):
    count, fields = (arrived.shape[1], arrived.shape[2])
    return (
        arrived.reshape(groups, count, fields, cols_own, slab)
        .transpose(1, 2, 3, 0, 4)
        .reshape(count, fields, cols_own, groups * slab)
    )


def columns_to_sending(stacked, groups, slab, cols_own):
    count, fields = (stacked.shape[0], stacked.shape[1])
    return (
        stacked.reshape(count, fields, cols_own, groups, slab)
        .transpose(3, 0, 1, 2, 4)
        .reshape(groups, count, fields, cols_own * slab)
    )


def landed_to_rows(landed, groups, slab, cols_own):
    count, fields = (landed.shape[1], landed.shape[2])
    return (
        landed.reshape(groups, count, fields, cols_own, slab)
        .transpose(1, 2, 4, 0, 3)
        .reshape(count, fields, slab, groups * cols_own)
    )


def local(block_tile, cell_index, masses, plane_coef, plane_dist, source_inv):
    groups = lax.axis_size("pix")
    my_index = lax.axis_index("pix")
    planes, local_tiles, per_tile = cell_index.shape
    slab = L // groups
    per_owner = slab // TR * (L // TC)
    cap = max(1, 2 * local_tiles // groups)
    flat = TR * TC
    batch_tiles = 8
    deposited = lax.map(
        deposit_group,
        (cell_index.reshape(-1, batch_tiles, per_tile), masses.reshape(-1, batch_tiles, per_tile)),
    )
    tile_sums = deposited.reshape(planes, local_tiles, flat)
    table = block_tile.reshape(planes, groups, local_tiles)
    owner = table // per_owner
    earlier = jnp.arange(local_tiles)[:, None] < jnp.arange(local_tiles)[None, :]
    same_owner = owner[:, :, :, None] == owner[:, :, None, :]
    rank = jnp.sum(jnp.where(same_owner & earlier[None, None], 1, 0), axis=2)
    slot = owner * cap + rank
    my_slots = lax.dynamic_index_in_dim(slot, my_index, axis=1, keepdims=False)
    slot_grid = jnp.arange(groups)[:, None] * cap + jnp.arange(cap)[None, :]
    send_hot = (my_slots[:, None, None, :] == slot_grid[None, :, :, None]).astype(jnp.float32)
    outgoing = jnp.einsum("pnct,ptf->npcf", send_hot, tile_sums, precision=HIGHEST)
    incoming = lax.all_to_all(outgoing, "pix", split_axis=0, concat_axis=0, tiled=True)
    local_index = table - my_index * per_owner
    is_mine = owner == my_index
    tile_hot = (is_mine[..., None] & (local_index[..., None] == jnp.arange(per_owner))).astype(
        jnp.float32
    )
    slot_hot = (rank[..., None] == jnp.arange(cap)).astype(jnp.float32)
    placing = jnp.einsum("pstl,pstc->plsc", tile_hot, slot_hot, precision=HIGHEST)
    slab_tiles = jnp.einsum("plsc,spcf->plf", placing, incoming, precision=HIGHEST)
    density = (
        slab_tiles.reshape(planes, slab // TR, L // TC, TR, TC)
        .transpose(0, 1, 3, 2, 4)
        .reshape(planes, slab, L)
    )
    total = lax.psum(jnp.sum(density, axis=(1, 2)), "pix")
    contrast = density / (total / (L * L))[:, None, None] - 1.0
    near_local = jnp.cumsum(plane_coef[:, None, None] * contrast, axis=0)
    far_local = jnp.cumsum((plane_coef * plane_dist)[:, None, None] * contrast, axis=0)
    blank = jnp.zeros((slab, L), jnp.float32)
    near_before, far_before = entering(
        (near_local[-1], far_local[-1]), "shell", add_pairs, (blank, blank)
    )
    convergence = near_before + near_local - source_inv[:, None, None] * (far_before + far_local)
    cols_own = L // groups
    wave_x, keep_x = frequency_of(my_index * cols_own + jnp.arange(cols_own), L)
    wave_y, keep_y = frequency_of(jnp.arange(L), L)
    wave_x = wave_x[:, None]
    wave_y = wave_y[None, :]
    both_keep = keep_x[:, None] * keep_y[None, :]
    wave_power = jnp.maximum(wave_x * wave_x + wave_y * wave_y, 1.0)
    kernel_one = both_keep * (wave_x * wave_x - wave_y * wave_y) / wave_power
    kernel_two = both_keep * 2.0 * wave_x * wave_y / wave_power
    scale = 1.0 / (L * L)
    spec_real, spec_imag = transform_last(convergence[0::2], convergence[1::2], -1.0)
    sending = rows_to_sending(jnp.stack([spec_real, spec_imag], axis=1), groups, slab, cols_own)
    arrived = lax.all_to_all(sending, "pix", split_axis=0, concat_axis=0, tiled=True)
    columns = arrived_to_columns(arrived, groups, slab, cols_own)
    row_real, row_imag = transform_last(columns[:, 0], columns[:, 1], -1.0)
    first_real, first_imag = transform_last(row_real * kernel_one, row_imag * kernel_one, 1.0)
    second_real, second_imag = transform_last(row_real * kernel_two, row_imag * kernel_two, 1.0)
    stacked = jnp.stack([first_real, first_imag, second_real, second_imag], axis=1)
    landed = lax.all_to_all(
        columns_to_sending(stacked, groups, slab, cols_own),
        "pix",
        split_axis=0,
        concat_axis=0,
        tiled=True,
    )
    row_layout = landed_to_rows(landed, groups, slab, cols_own)
    even_one, odd_one = transform_last(row_layout[:, 0], row_layout[:, 1], 1.0)
    even_two, odd_two = transform_last(row_layout[:, 2], row_layout[:, 3], 1.0)
    shear_one = jnp.stack([even_one, odd_one], axis=1).reshape(planes, slab, L)
    shear_two = jnp.stack([even_two, odd_two], axis=1).reshape(planes, slab, L)
    return (convergence, shear_one * scale, shear_two * scale)


def solution(mesh):
    placed = (
        P("shell", None),
        P("shell", "pix", None),
        P("shell", "pix", None),
        P("shell"),
        P("shell"),
        P("shell"),
    )
    return jax.shard_map(
        local,
        mesh=mesh,
        in_specs=placed,
        out_specs=(P("shell", "pix", None), P("shell", "pix", None), P("shell", "pix", None)),
        check_vma=False,
    )
```

profile of v0, /device:TPU:1, one launch (start us, length us, event | category | flops | bytes accessed | tf_op | source)
XLA Modules:
  0.0 498.4 jit_solution(13083244063688740668)
XLA Ops:
  8.0 56.0 %while.8 = (s32[]{:T(128)}, f32[16,8,16,128]{3,2,1,0:T(8,128)S(1)}, s32[16,8,512]{2,1,0:T(8,128)}, bf16[16,8,512]{2,1,0:T(8,128)(2,1)}, s32[]{:T(128)}) while((s32[]{:T(128)}, f32[16,8,16,128]{3,2,1,0:T(8,128)S(1)}, s32[16,8,512]{2,1,0:T(8,128)}, bf16[16,8,512]{2,1,0:T(8,128)(2,1)}, s32[]{:T(128)}) %tuple.63), condition=%wide.region_2.3_spmd, body=%wide.region_1.2_spmd.sunk | while | flops 17534976 | bytes 196693 | solution.py:150
  65.7 2.5 copy.183
  68.2 7.3 %all-to-all-start = ((f32[16,2,8,2048]{3,2,1,0:T(8,128)}), f32[16,2,8,2048]{3,2,1,0:T(8,128)S(1)}, u32[]{:S(2)}, u32[]{:S(2)}) async-start(f32[16,2,8,2048]{3,2,1,0:T(8,128)} %copy.183), calls=%async_computation | async-start | bytes 4194304 | tf_op jit(solution)/shard_map/all_to_all | solution.py:165
  76.9 40.2 %all-to-all-done = f32[16,2,8,2048]{3,2,1,0:T(8,128)S(1)} async-done(((f32[16,2,8,2048]{3,2,1,0:T(8,128)}), f32[16,2,8,2048]{3,2,1,0:T(8,128)S(1)}, u32[]{:S(2)}, u32[]{:S(2)}) %all-to-all-start) | async-done | bytes 2097184 | tf_op jit(solution)/shard_map/all_to_all | solution.py:165
  117.1 3.2 bitcast_reduce_fusion
  120.3 33.9 %psum.7 = f32[2]{0:T(128)S(1)} all-reduce(f32[2]{0:T(128)S(1)} %get-tuple-element.117), channel_id=1, replica_groups=mesh['shell'=2,'pix'=16] {'pix'}, use_global_device_ids=true, to_apply=%region_4.5 | all-reduce | flops 2 | bytes 16 | tf_op jit(solution)/shard_map/psum | solution.py:179
  154.2 2.0 copy.236
  156.2 2.0 copy.185
  158.2 1.7 reshape.931
  165.7 31.5 %all-gather.3.cloned.1.call-done = f32[2,128,2048]{2,1,0:T(8,128)} async-done(((f32[1,128,2048]{2,1,0:T(8,128)}), f32[2,128,2048]{2,1,0:T(8,128)}) %all-gather.3.cloned.1.call-update) | async-done | bytes 2097168 | tf_op jit(solution)/shard_map/all_gather | solution.py:16
  198.6 33.9 %all-gather.5.cloned.1.call-done = f32[2,128,2048]{2,1,0:T(8,128)} async-done(((f32[1,128,2048]{2,1,0:T(8,128)}), f32[2,128,2048]{2,1,0:T(8,128)}) %all-gather.5.cloned.1.call-update) | async-done | bytes 2097168 | tf_op jit(solution)/shard_map/all_gather | solution.py:16
  245.7 2.0 fusion.31
  247.9 1.8 copy.190
  249.7 6.4 %all-to-all-start.1 = ((f32[16,1,2,16384]{3,1,2,0:T(1,128)}), f32[16,1,2,16384]{3,1,2,0:T(1,128)S(1)}, u32[]{:S(2)}, u32[]{:S(2)}) async-start(f32[16,1,2,16384]{3,1,2,0:T(1,128)} %bitcast.319), calls=%async_computation.1 | async-start | bytes 4194304 | tf_op jit(solution)/shard_map/all_to_all | solution.py:200
  256.2 41.4 %all-to-all-done.1 = f32[16,1,2,16384]{3,1,2,0:T(1,128)S(1)} async-done(((f32[16,1,2,16384]{3,1,2,0:T(1,128)}), f32[16,1,2,16384]{3,1,2,0:T(1,128)S(1)}, u32[]{:S(2)}, u32[]{:S(2)}) %all-to-all-start.1) | async-done | bytes 2097184 | tf_op jit(solution)/shard_map/all_to_all | solution.py:200
  297.6 1.8 copy.191
  299.4 2.6 fusion.465
  304.7 1.7 copy.235
  314.4 1.6 fusion.97
  324.5 1.9 multiply_add_fusion.3
  326.4 2.0 fusion.65
  328.4 1.6 fusion.67
  330.0 1.6 fusion.59
  331.6 1.6 fusion.61
  333.3 1.6 fusion.28
  334.9 1.6 fusion.27
  336.6 1.6 fusion.26
  338.2 1.8 fusion.25
  341.7 103.1 %all_to_all.15 = f32[16,1,4,16384]{3,1,2,0:T(1,128)S(1)} all-to-all(f32[16,1,4,16384]{3,1,2,0:T(1,128)S(1)} %bitcast.304), channel_id=1, replica_groups=mesh['shell'=2,'pix'=16] {'pix'}, dimensions={0} | all-to-all | bytes 8388608 | tf_op jit(solution)/shard_map/all_to_all | solution.py:206
  445.6 1.9 fusion.91
  447.6 1.9 fusion.108
  449.5 1.9 fusion.94
  451.4 1.9 fusion.111
  453.4 2.0 convolution_subtract_fusion.3
  455.4 2.2 convolution_add_fusion.3
  457.5 2.0 convolution_subtract_fusion.1
  459.5 2.3 multiply_add_fusion
  461.8 1.6 fusion.47
  463.4 1.6 fusion.49
  465.1 1.6 fusion.53
  466.7 1.6 fusion.55
  468.3 2.8 fusion.22
  471.2 2.6 fusion.21
  473.8 2.4 stack_reshape.21
  476.2 2.4 stack_reshape.20
  478.5 2.6 fusion.24
  481.1 2.6 fusion.23
  483.7 2.5 stack_reshape.9
  (154 shorter events, 106.5 us)
Async XLA Ops:
  68.2 48.9 %all-to-all-start = ((f32[16,2,8,2048]{3,2,1,0:T(8,128)}), f32[16,2,8,2048]{3,2,1,0:T(8,128)S(1)}, u32[]{:S(2)}, u32[]{:S(2)}) async-start(f32[16,2,8,2048]{3,2,1,0:T(8,128)} %copy.183), calls=%async_computation | async-start | bytes 4194304 | tf_op jit(solution)/shard_map/all_to_all | solution.py:165
  75.6 121.7 %all-gather.3.cloned.1.call-start = ((), (), s32[]{:S(2)}) async-start(), calls=%async_computation.3 | async-start | bytes 3145728 | tf_op jit(solution)/shard_map/all_gather | solution.py:16
  158.2 1.7 copy-start.10
  160.2 1.3 copy-start
  161.6 1.4 copy-start.12
  162.7 69.9 %all-gather.5.cloned.1.call-start = ((), (), s32[]{:S(2)}) async-start(), calls=%async_computation.4 | async-start | bytes 3145728 | tf_op jit(solution)/shard_map/all_gather | solution.py:16
  163.3 1.3 copy-start.2
  165.7 68.3 %copy-start.1 = (f32[2,128,2048]{2,1,0:T(8,128)S(1)}, f32[2,128,2048]{2,1,0:T(8,128)}, u32[]{:S(2)}) copy-start(f32[2,128,2048]{2,1,0:T(8,128)} %copy-done) | copy-start | bytes 6291460
  165.7 68.3 %copy-start.11 = (f32[2]{0:T(128)S(1)}, f32[2]{0:T(128)}, u32[]{:S(2)}) copy-start(f32[2]{0:T(128)} %param.13) | copy-start | bytes 28
  232.5 1.9 copy-start.3
  235.1 1.3 copy-start.4
  249.7 47.9 %all-to-all-start.1 = ((f32[16,1,2,16384]{3,1,2,0:T(1,128)}), f32[16,1,2,16384]{3,1,2,0:T(1,128)S(1)}, u32[]{:S(2)}, u32[]{:S(2)}) async-start(f32[16,1,2,16384]{3,1,2,0:T(1,128)} %bitcast.319), calls=%async_computation.1 | async-start | bytes 4194304 | tf_op jit(solution)/shard_map/all_to_all | solution.py:200
  481.1 5.1 %copy-start.5 = (f32[1,128,16,128]{3,2,1,0:T(8,128)S(1)}, f32[1,128,16,128]{3,2,1,0:T(8,128)}, u32[]{:S(2)}) copy-start(f32[1,128,16,128]{3,2,1,0:T(8,128)} %fusion.24) | copy-start | bytes 3145732
  483.7 3.7 copy-start.6
  483.7 3.7 copy-start.7
  487.4 1.5 copy-start.8
  487.4 2.3 copy-start.9
Sparse Core Ops, SparseCore 0:
  162.8 34.4 all-gather.2
  199.4 33.0 all-gather.4
where the time goes:
time: 508 us; the launch traced here: 498 us
  waiting for transfers between devices  147 us (29%)
  blocking collectives  137 us (27%)
  matrix products  106 us (21%)
  local copies, waits for them, and re-layouts  47.2 us (9%)
  other arithmetic  31.7 us (6%)
  between operations  15.1 us (3%)
  starting transfers between devices  14 us (3%)
    all_to_all x1, blocking collectives, local(): lax.all_to_all(columns_to_sending(stacked, groups, slab, cols_own), 'pix'...  103 us
    all_gather x2, waiting for transfers between devices, entering(): pieces = jax.tree.map(lambda part: lax.all_gather(part, axis), value)  65.5 us
    all_to_all x1, waiting for transfers between devices, local(): lax.all_to_all(sending, 'pix', split_axis=0, concat_axis=0, tiled=True)  41.4 us
    all_to_all x1, waiting for transfers between devices, local(): lax.all_to_all(outgoing, 'pix', split_axis=0, concat_axis=0, tiled=True)  40.2 us
    psum x1, blocking collectives, local(): total = lax.psum(jnp.sum(density, axis=(1, 2)), 'pix')  33.9 us
    dot_general x16, matrix products, deposit_group(): jnp.einsum('grk,gkc->grc', row_hot, col_hot, preferred_element_type=jnp.f...  21.1 us
    select_n x16, other arithmetic, deposit_group(): tile_cols = cell_ids % TC  11.7 us
    select_n x16, other arithmetic, deposit_group(): tile_rows = cell_ids // TC  11.7 us
  transfers between devices with their start and end apart: 4, of which 4 were waited for; matrix products, arithmetic and copies ran while one was open for 1% of the time, Pallas kernels for 0%

commit v1 on v0

--- a/solution.py
+++ b/solution.py
@@ -9,6 +9,18 @@
 TR = 16
 TC = 128
 HIGHEST = lax.Precision.HIGHEST
+
+
+def rotated_exchange(array, axis, split, join):
+    ways, here = (lax.axis_size(axis), lax.axis_index(axis))
+    width = array.shape[split] // ways
+    turned = jnp.roll(array, -here * width, axis=split)
+    got = [lax.slice_in_dim(turned, 0, width, axis=split)]
+    for far in range(1, ways):
+        sent = lax.slice_in_dim(turned, far * width, (far + 1) * width, axis=split)
+        got.append(lax.ppermute(sent, axis, [(d, (d + far) % ways) for d in range(ways)]))
+    line = jnp.concatenate(got[::-1], axis=join)
+    return jnp.roll(line, (here + 1) * got[0].shape[join], axis=join)
 
 
 def entering(value, axis, join, neutral):
@@ -197,7 +209,7 @@
     scale = 1.0 / (L * L)
     spec_real, spec_imag = transform_last(convergence[0::2], convergence[1::2], -1.0)
     sending = rows_to_sending(jnp.stack([spec_real, spec_imag], axis=1), groups, slab, cols_own)
-    arrived = lax.all_to_all(sending, "pix", split_axis=0, concat_axis=0, tiled=True)
+    arrived = rotated_exchange(sending, "pix", 0, 0)
     columns = arrived_to_columns(arrived, groups, slab, cols_own)
     row_real, row_imag = transform_last(columns[:, 0], columns[:, 1], -1.0)
     first_real, first_imag = transform_last(row_real * kernel_one, row_imag * kernel_one, 1.0)

time: 508 us -> 549 us (1.081)
  starting transfers between devices: 14 us -> 38.6 us
  other arithmetic: 31.7 us -> 47.1 us
  blocking collectives: 137 us -> 131 us
    ppermute x0 -> x15, waiting for transfers between devices: none -> 47.9 us  [rotated_exchange(): lax.ppermute(sent, axis, [(d, (d + far) % ways) for d in range(ways)])]
    all_to_all x1 -> x0, waiting for transfers between devices: 41.4 us -> none  [local(): lax.all_to_all(sending, 'pix', split_axis=0, concat_axis=0, tiled=True)]
    ppermute x0 -> x15, starting transfers between devices: none -> 30.9 us  [rotated_exchange(): lax.ppermute(sent, axis, [(d, (d + far) % ways) for d in range(ways)])]
    concatenate x0 -> x2, other arithmetic: none -> 12.5 us  [the longest x1 6.67 us: rotated_exchange(): turned = jnp.roll(array, -here * width, axis=split)]
    all_to_all x1 -> x0, starting transfers between devices: 6.38 us -> none  [local(): lax.all_to_all(sending, 'pix', split_axis=0, concat_axis=0, tiled=True)]
    all_to_all x1, blocking collectives: 103 us -> 97.5 us  [local(): lax.all_to_all(columns_to_sending(stacked, groups, slab, cols_own), 'pix'...]
  transfers between devices with their start and end apart: 4 -> 18, of which waited for: 4 -> 13; matrix products, arithmetic and copies ran while one was open for 1% -> 2% of each run, Pallas kernels for 0% -> 0%
where the time goes in v1:
time: 549 us; the launch traced here: 539 us
  waiting for transfers between devices  152 us (28%)
  blocking collectives  131 us (24%)
  matrix products  106 us (19%)
  local copies, waits for them, and re-layouts  48.1 us (9%)
  other arithmetic  47.1 us (9%)
  starting transfers between devices  38.6 us (7%)
  between operations  15.4 us (3%)
    all_to_all x1, blocking collectives, local(): lax.all_to_all(columns_to_sending(stacked, groups, slab, cols_own), 'pix'...  97.5 us
    all_gather x2, waiting for transfers between devices, entering(): pieces = jax.tree.map(lambda part: lax.all_gather(part, axis), value)  63.7 us
    ppermute x15, waiting for transfers between devices, rotated_exchange(): lax.ppermute(sent, axis, [(d, (d + far) % ways) for d in range(ways)])  47.9 us
    all_to_all x1, waiting for transfers between devices, local(): lax.all_to_all(outgoing, 'pix', split_axis=0, concat_axis=0, tiled=True)  40.2 us
    psum x1, blocking collectives, local(): total = lax.psum(jnp.sum(density, axis=(1, 2)), 'pix')  33.9 us
    ppermute x15, starting transfers between devices, rotated_exchange(): lax.ppermute(sent, axis, [(d, (d + far) % ways) for d in range(ways)])  30.9 us
    dot_general x16, matrix products, deposit_group(): jnp.einsum('grk,gkc->grc', row_hot, col_hot, preferred_element_type=jnp.f...  21.1 us
    select_n x16, other arithmetic, deposit_group(): tile_cols = cell_ids % TC  11.7 us
  transfers between devices with their start and end apart: 18, of which 13 were waited for; matrix products, arithmetic and copies ran while one was open for 2% of the time, Pallas kernels for 0%

profile of v1, /device:TPU:1, one launch (start us, length us, event | category | flops | bytes accessed | tf_op | source)
XLA Modules:
  0.0 538.8 jit_solution(9536464123188302767)
XLA Ops:
  8.0 56.0 %while.8 = (s32[]{:T(128)}, f32[16,8,16,128]{3,2,1,0:T(8,128)S(1)}, s32[16,8,512]{2,1,0:T(8,128)}, bf16[16,8,512]{2,1,0:T(8,128)(2,1)}, s32[]{:T(128)}) while((s32[]{:T(128)}, f32[16,8,16,128]{3,2,1,0:T(8,128)S(1)}, s32[16,8,512]{2,1,0:T(8,128)}, bf16[16,8,512]{2,1,0:T(8,128)(2,1)}, s32[]{:T(128)}) %tuple.78), condition=%wide.region_2.3_spmd, body=%wide.region_1.2_spmd.sunk | while | flops 17534976 | bytes 196693 | solution.py:162
  65.7 2.5 copy.183
  68.2 7.3 %all-to-all-start = ((f32[16,2,8,2048]{3,2,1,0:T(8,128)}), f32[16,2,8,2048]{3,2,1,0:T(8,128)S(1)}, u32[]{:S(2)}, u32[]{:S(2)}) async-start(f32[16,2,8,2048]{3,2,1,0:T(8,128)} %copy.183), calls=%async_computation | async-start | bytes 4194304 | tf_op jit(solution)/shard_map/all_to_all | solution.py:177
  76.9 40.2 %all-to-all-done = f32[16,2,8,2048]{3,2,1,0:T(8,128)S(1)} async-done(((f32[16,2,8,2048]{3,2,1,0:T(8,128)}), f32[16,2,8,2048]{3,2,1,0:T(8,128)S(1)}, u32[]{:S(2)}, u32[]{:S(2)}) %all-to-all-start) | async-done | bytes 2097184 | tf_op jit(solution)/shard_map/all_to_all | solution.py:177
  117.1 3.2 bitcast_reduce_fusion
  120.3 33.9 %psum.7 = f32[2]{0:T(128)S(1)} all-reduce(f32[2]{0:T(128)S(1)} %get-tuple-element.133), channel_id=1, replica_groups=mesh['shell'=2,'pix'=16] {'pix'}, use_global_device_ids=true, to_apply=%region_4.5 | all-reduce | flops 2 | bytes 16 | tf_op jit(solution)/shard_map/psum | solution.py:191
  154.2 2.0 copy.236
  156.2 2.0 copy.185
  167.5 29.7 %all-gather.3.cloned.1.call-done = f32[2,128,2048]{2,1,0:T(8,128)} async-done(((f32[1,128,2048]{2,1,0:T(8,128)}), f32[2,128,2048]{2,1,0:T(8,128)}) %all-gather.3.cloned.1.call-update) | async-done | bytes 2097168 | tf_op jit(solution)/shard_map/all_gather | solution.py:28
  198.6 33.9 %all-gather.5.cloned.1.call-done = f32[2,128,2048]{2,1,0:T(8,128)} async-done(((f32[1,128,2048]{2,1,0:T(8,128)}), f32[2,128,2048]{2,1,0:T(8,128)}) %all-gather.5.cloned.1.call-update) | async-done | bytes 2097168 | tf_op jit(solution)/shard_map/all_gather | solution.py:28
  245.7 2.0 fusion.33
  249.7 6.7 %fusion.14 = f32[16,1,2,16384]{3,1,2,0:T(1,128)S(1)} fusion(s32[]{:T(128)S(6)} %select_n.400, f32[16,1,2,16384]{3,1,2,0:T(1,128)} %bitcast.320), kind=kLoop, calls=%fused_computation.29 | loop fusion | flops 524288 | bytes 4194308 | tf_op jit(solution)/shard_map/jit(_roll_dynamic)/concatenate | solution.py:17
  260.4 1.9 collective-permute-start.13
  263.7 6.1 %collective-permute-start.1 = (f32[1,1,2,16384]{3,1,2,0:T(1,128)}, f32[1,1,2,16384]{3,1,2,0:T(1,128)S(1)}, u32[]{:S(2)}, u32[]{:S(2)}) collective-permute-start(f32[1,1,2,16384]{3,1,2,0:T(1,128)} %get-tuple-element.125), channel_id=1, source_target_pairs={{0,14},{1,15},{2,0},{3,1},{4,2},{5,3},{6,4},{7,5},{8,6},{9,7},{10,... | collective-permute-start | bytes 393224 | tf_op jit(solution)/shard_map/ppermute | solution.py:21
  272.5 4.1 collective-permute-start.2
  276.7 2.8 collective-permute-done.2
  279.5 2.8 collective-permute-start.3
  282.3 2.3 collective-permute-done.3
  284.6 2.9 collective-permute-start.4
  287.5 3.2 collective-permute-done.4
  290.7 3.9 collective-permute-start.5
  294.6 2.2 collective-permute-done.5
  296.8 3.1 collective-permute-start.6
  300.0 7.3 %collective-permute-done.6 = f32[1,1,2,16384]{3,1,2,0:T(1,128)S(1)} collective-permute-done((f32[1,1,2,16384]{3,1,2,0:T(1,128)S(1)}, f32[1,1,2,16384]{3,1,2,0:T(1,128)S(1)}, u32[]{:S(2)}, u32[]{:S(2)}) %collective-permute-start.6) | collective-permute-done | bytes 131104 | tf_op jit(solution)/shard_map/ppermute | solution.py:21
  308.2 6.6 %collective-permute-done.7 = f32[1,1,2,16384]{3,1,2,0:T(1,128)S(1)} collective-permute-done((f32[1,1,2,16384]{3,1,2,0:T(1,128)S(1)}, f32[1,1,2,16384]{3,1,2,0:T(1,128)S(1)}, u32[]{:S(2)}, u32[]{:S(2)}) %collective-permute-start.7) | collective-permute-done | bytes 131104 | tf_op jit(solution)/shard_map/ppermute | solution.py:21
  314.9 9.6 %collective-permute-done.8 = f32[1,1,2,16384]{3,1,2,0:T(1,128)S(1)} collective-permute-done((f32[1,1,2,16384]{3,1,2,0:T(1,128)S(1)}, f32[1,1,2,16384]{3,1,2,0:T(1,128)S(1)}, u32[]{:S(2)}, u32[]{:S(2)}) %collective-permute-start.8) | collective-permute-done | bytes 131104 | tf_op jit(solution)/shard_map/ppermute | solution.py:21
  325.3 6.3 %collective-permute-done.9 = f32[1,1,2,16384]{3,1,2,0:T(1,128)S(1)} collective-permute-done((f32[1,1,2,16384]{3,1,2,0:T(1,128)S(1)}, f32[1,1,2,16384]{3,1,2,0:T(1,128)S(1)}, u32[]{:S(2)}, u32[]{:S(2)}) %collective-permute-start.9) | collective-permute-done | bytes 131104 | tf_op jit(solution)/shard_map/ppermute | solution.py:21
  332.7 5.7 %collective-permute-done.10 = f32[1,1,2,16384]{3,1,2,0:T(1,128)S(1)} collective-permute-done((f32[1,1,2,16384]{3,1,2,0:T(1,128)S(1)}, f32[1,1,2,16384]{3,1,2,0:T(1,128)S(1)}, u32[]{:S(2)}, u32[]{:S(2)}) %collective-permute-start.10) | collective-permute-done | bytes 131104 | tf_op jit(solution)/shard_map/ppermute | solution.py:21
  338.6 5.8 %fusion.13 = f32[16,1,2,16384]{3,1,2,0:T(1,128)} fusion(s32[]{:T(128)S(6)} %select_n.402, f32[16,1,2,16384]{3,1,2,0:T(1,128)S(1)} %slice_dynamic-update-slice_fusion), kind=kLoop, calls=%fused_computation.28 | loop fusion | flops 524288 | bytes 4194308 | tf_op jit(solution)/shard_map/jit(_roll_dynamic)/concatenate | solution.py:23
  344.5 2.1 copy.191
  370.3 1.9 multiply_add_fusion.3
  372.2 2.1 fusion.67
  387.6 97.5 %all_to_all.10 = f32[16,1,4,16384]{3,1,2,0:T(1,128)S(1)} all-to-all(f32[16,1,4,16384]{3,1,2,0:T(1,128)S(1)} %bitcast.304), channel_id=1, replica_groups=mesh['shell'=2,'pix'=16] {'pix'}, dimensions={0} | all-to-all | bytes 8388608 | tf_op jit(solution)/shard_map/all_to_all | solution.py:218
  485.9 1.9 fusion.93
  487.9 1.9 fusion.110
  489.8 1.9 fusion.96
  491.8 1.9 fusion.113
  493.7 2.0 convolution_subtract_fusion.3
  495.7 2.2 convolution_add_fusion.3
  497.9 2.0 convolution_subtract_fusion.1
  499.8 2.3 multiply_add_fusion
  508.7 2.8 fusion.24
  511.5 2.6 fusion.23
  514.1 2.4 stack_reshape.21
  516.5 2.4 stack_reshape.20
  518.8 2.6 fusion.26
  521.5 2.6 fusion.25
  524.1 2.5 stack_reshape.9
  (215 shorter events, 145.4 us)
Async XLA Ops:
  68.2 48.9 %all-to-all-start = ((f32[16,2,8,2048]{3,2,1,0:T(8,128)}), f32[16,2,8,2048]{3,2,1,0:T(8,128)S(1)}, u32[]{:S(2)}, u32[]{:S(2)}) async-start(f32[16,2,8,2048]{3,2,1,0:T(8,128)} %copy.183), calls=%async_computation | async-start | bytes 4194304 | tf_op jit(solution)/shard_map/all_to_all | solution.py:177
  75.6 121.7 %all-gather.3.cloned.1.call-start = ((), (), s32[]{:S(2)}) async-start(), calls=%async_computation.2 | async-start | bytes 3145728 | tf_op jit(solution)/shard_map/all_gather | solution.py:28
  158.2 1.7 copy-start.14
  160.2 1.3 copy-start
  161.6 1.4 copy-start.18
  162.7 69.9 %all-gather.5.cloned.1.call-start = ((), (), s32[]{:S(2)}) async-start(), calls=%async_computation.3 | async-start | bytes 3145728 | tf_op jit(solution)/shard_map/all_gather | solution.py:28
  163.3 1.3 copy-start.2
  167.5 66.5 %copy-start.1 = (f32[2,128,2048]{2,1,0:T(8,128)S(1)}, f32[2,128,2048]{2,1,0:T(8,128)}, u32[]{:S(2)}) copy-start(f32[2,128,2048]{2,1,0:T(8,128)} %copy-done) | copy-start | bytes 6291460
  167.5 66.5 %copy-start.15 = (f32[2]{0:T(128)S(1)}, f32[2]{0:T(128)}, u32[]{:S(2)}) copy-start(f32[2]{0:T(128)} %param.15) | copy-start | bytes 28
  232.5 1.9 copy-start.3
  235.1 1.3 copy-start.4
  257.3 6.4 %collective-permute-start = (f32[1,1,2,16384]{3,1,2,0:T(1,128)}, f32[1,1,2,16384]{3,1,2,0:T(1,128)}, u32[]{:S(2)}, u32[]{:S(2)}) collective-permute-start(f32[1,1,2,16384]{3,1,2,0:T(1,128)} %get-tuple-element.126), channel_id=1, source_target_pairs={{0,15},{1,0},{2,1},{3,2},{4,3},{5,4},{6,5},{7,6},{8,7},{9,8},{10,9... | collective-permute-start | bytes 393224 | tf_op jit(solution)/shard_map/ppermute | solution.py:21
  259.4 79.1 %collective-permute-start.14 = (f32[1,1,2,16384]{3,1,2,0:T(1,128)S(1)}, f32[1,1,2,16384]{3,1,2,0:T(1,128)S(1)}, u32[]{:S(2)}, u32[]{:S(2)}) collective-permute-start(f32[1,1,2,16384]{3,1,2,0:T(1,128)S(1)} %get-tuple-element.112), channel_id=1, source_target_pairs={{0,1},{1,2},{2,3},{3,4},{4,5},{5,6},{6,7},{7,8},{8,9},{9,10},{10,1... | collective-permute-start | bytes 393224 | tf_op jit(solution)/shard_map/ppermute | solution.py:21
  260.4 78.1 %collective-permute-start.13 = (f32[1,1,2,16384]{3,1,2,0:T(1,128)S(1)}, f32[1,1,2,16384]{3,1,2,0:T(1,128)S(1)}, u32[]{:S(2)}, u32[]{:S(2)}) collective-permute-start(f32[1,1,2,16384]{3,1,2,0:T(1,128)S(1)} %get-tuple-element.113), channel_id=1, source_target_pairs={{0,2},{1,3},{2,4},{3,5},{4,6},{5,7},{6,8},{7,9},{8,10},{9,11},{10,... | collective-permute-start | bytes 393224 | tf_op jit(solution)/shard_map/ppermute | solution.py:21
  262.3 76.2 %collective-permute-start.12 = (f32[1,1,2,16384]{3,1,2,0:T(1,128)S(1)}, f32[1,1,2,16384]{3,1,2,0:T(1,128)S(1)}, u32[]{:S(2)}, u32[]{:S(2)}) collective-permute-start(f32[1,1,2,16384]{3,1,2,0:T(1,128)S(1)} %get-tuple-element.114), channel_id=1, source_target_pairs={{0,3},{1,4},{2,5},{3,6},{4,7},{5,8},{6,9},{7,10},{8,11},{9,12},{10... | collective-permute-start | bytes 393224 | tf_op jit(solution)/shard_map/ppermute | solution.py:21
  262.4 76.0 %collective-permute-start.11 = (f32[1,1,2,16384]{3,1,2,0:T(1,128)S(1)}, f32[1,1,2,16384]{3,1,2,0:T(1,128)S(1)}, u32[]{:S(2)}, u32[]{:S(2)}) collective-permute-start(f32[1,1,2,16384]{3,1,2,0:T(1,128)S(1)} %get-tuple-element.115), channel_id=1, source_target_pairs={{0,4},{1,5},{2,6},{3,7},{4,8},{5,9},{6,10},{7,11},{8,12},{9,13},{1... | collective-permute-start | bytes 393224 | tf_op jit(solution)/shard_map/ppermute | solution.py:21
  263.7 8.8 %collective-permute-start.1 = (f32[1,1,2,16384]{3,1,2,0:T(1,128)}, f32[1,1,2,16384]{3,1,2,0:T(1,128)S(1)}, u32[]{:S(2)}, u32[]{:S(2)}) collective-permute-start(f32[1,1,2,16384]{3,1,2,0:T(1,128)} %get-tuple-element.125), channel_id=1, source_target_pairs={{0,14},{1,15},{2,0},{3,1},{4,2},{5,3},{6,4},{7,5},{8,6},{9,7},{10,... | collective-permute-start | bytes 393224 | tf_op jit(solution)/shard_map/ppermute | solution.py:21
  272.5 7.0 %collective-permute-start.2 = (f32[1,1,2,16384]{3,1,2,0:T(1,128)}, f32[1,1,2,16384]{3,1,2,0:T(1,128)S(1)}, u32[]{:S(2)}, u32[]{:S(2)}) collective-permute-start(f32[1,1,2,16384]{3,1,2,0:T(1,128)} %get-tuple-element.124), channel_id=1, source_target_pairs={{0,13},{1,14},{2,15},{3,0},{4,1},{5,2},{6,3},{7,4},{8,5},{9,6},{10... | collective-permute-start | bytes 393224 | tf_op jit(solution)/shard_map/ppermute | solution.py:21
  279.5 5.1 collective-permute-start.3
  284.6 6.1 %collective-permute-start.4 = (f32[1,1,2,16384]{3,1,2,0:T(1,128)S(1)}, f32[1,1,2,16384]{3,1,2,0:T(1,128)S(1)}, u32[]{:S(2)}, u32[]{:S(2)}) collective-permute-start(f32[1,1,2,16384]{3,1,2,0:T(1,128)S(1)} %get-tuple-element.122), channel_id=1, source_target_pairs={{0,11},{1,12},{2,13},{3,14},{4,15},{5,0},{6,1},{7,2},{8,3},{9,4},{... | collective-permute-start | bytes 393224 | tf_op jit(solution)/shard_map/ppermute | solution.py:21
  290.7 6.1 %collective-permute-start.5 = (f32[1,1,2,16384]{3,1,2,0:T(1,128)S(1)}, f32[1,1,2,16384]{3,1,2,0:T(1,128)S(1)}, u32[]{:S(2)}, u32[]{:S(2)}) collective-permute-start(f32[1,1,2,16384]{3,1,2,0:T(1,128)S(1)} %get-tuple-element.121), channel_id=1, source_target_pairs={{0,10},{1,11},{2,12},{3,13},{4,14},{5,15},{6,0},{7,1},{8,2},{9,3},... | collective-permute-start | bytes 393224 | tf_op jit(solution)/shard_map/ppermute | solution.py:21
  296.8 10.5 %collective-permute-start.6 = (f32[1,1,2,16384]{3,1,2,0:T(1,128)S(1)}, f32[1,1,2,16384]{3,1,2,0:T(1,128)S(1)}, u32[]{:S(2)}, u32[]{:S(2)}) collective-permute-start(f32[1,1,2,16384]{3,1,2,0:T(1,128)S(1)} %get-tuple-element.120), channel_id=1, source_target_pairs={{0,9},{1,10},{2,11},{3,12},{4,13},{5,14},{6,15},{7,0},{8,1},{9,2},... | collective-permute-start | bytes 393224 | tf_op jit(solution)/shard_map/ppermute | solution.py:21
  307.3 7.5 %collective-permute-start.7 = (f32[1,1,2,16384]{3,1,2,0:T(1,128)S(1)}, f32[1,1,2,16384]{3,1,2,0:T(1,128)S(1)}, u32[]{:S(2)}, u32[]{:S(2)}) collective-permute-start(f32[1,1,2,16384]{3,1,2,0:T(1,128)S(1)} %get-tuple-element.119), channel_id=1, source_target_pairs={{0,8},{1,9},{2,10},{3,11},{4,12},{5,13},{6,14},{7,15},{8,0},{9,1},... | collective-permute-start | bytes 393224 | tf_op jit(solution)/shard_map/ppermute | solution.py:21
  314.8 9.7 %collective-permute-start.8 = (f32[1,1,2,16384]{3,1,2,0:T(1,128)S(1)}, f32[1,1,2,16384]{3,1,2,0:T(1,128)S(1)}, u32[]{:S(2)}, u32[]{:S(2)}) collective-permute-start(f32[1,1,2,16384]{3,1,2,0:T(1,128)S(1)} %get-tuple-element.118), channel_id=1, source_target_pairs={{0,7},{1,8},{2,9},{3,10},{4,11},{5,12},{6,13},{7,14},{8,15},{9,0},... | collective-permute-start | bytes 393224 | tf_op jit(solution)/shard_map/ppermute | solution.py:21
  324.5 7.1 %collective-permute-start.9 = (f32[1,1,2,16384]{3,1,2,0:T(1,128)S(1)}, f32[1,1,2,16384]{3,1,2,0:T(1,128)S(1)}, u32[]{:S(2)}, u32[]{:S(2)}) collective-permute-start(f32[1,1,2,16384]{3,1,2,0:T(1,128)S(1)} %get-tuple-element.117), channel_id=1, source_target_pairs={{0,6},{1,7},{2,8},{3,9},{4,10},{5,11},{6,12},{7,13},{8,14},{9,15},... | collective-permute-start | bytes 393224 | tf_op jit(solution)/shard_map/ppermute | solution.py:21
  331.6 6.8 %collective-permute-start.10 = (f32[1,1,2,16384]{3,1,2,0:T(1,128)S(1)}, f32[1,1,2,16384]{3,1,2,0:T(1,128)S(1)}, u32[]{:S(2)}, u32[]{:S(2)}) collective-permute-start(f32[1,1,2,16384]{3,1,2,0:T(1,128)S(1)} %get-tuple-element.116), channel_id=1, source_target_pairs={{0,5},{1,6},{2,7},{3,8},{4,9},{5,10},{6,11},{7,12},{8,13},{9,14},{... | collective-permute-start | bytes 393224 | tf_op jit(solution)/shard_map/ppermute | solution.py:21
  357.3 1.5 copy-start.11
  357.3 1.5 copy-start.12
  357.3 1.5 copy-start.16
  357.3 1.5 copy-start.17
  358.8 1.4 copy-start.13
  358.8 1.4 copy-start.19
  368.9 1.4 copy-start.10
  521.5 5.1 copy-start.5
  524.1 3.7 copy-start.6
  524.1 3.7 copy-start.7
  527.7 1.5 copy-start.8
  527.7 2.3 copy-start.9
Sparse Core Ops, SparseCore 0:
  162.8 34.4 all-gather.2
  199.4 33.0 all-gather.4
